TPU v7x, 256 devices: a whole 4x4x8 slice. The times are simulated.
256 devices in a mesh: section: 16 (over y, z_hi, core), dp: 16 (over x, z_lo).
Axes of the slice: x: 4, y: 4, z: 8 (z_hi: 2, z_lo: 4; z = z_hi * 4 + z_lo), core: 2. Of those that a mesh axis runs over, the one named last changes fastest.
Arguments:
- student_states: bfloat16 [16, 2048, 2048], P('section', 'dp'), may hold values from -6 to 6
- teacher_states: bfloat16 [64, 2048, 7168], P('section', 'dp'), may hold values from -18 to 18
- projector: bfloat16 [16, 2048, 7168], P('section', None, 'dp'), may hold values from -0.125 to 0.125
- layer_map: int32 [16], replicated, may hold values from 0 to 60, as said below
- boundaries: int32 [17], replicated, may hold values from 0 to 61, as said below
- valid_counts: int32 [16], P('dp'), may hold values from 32 to 128, as said below
Outputs:
- student_grads: bfloat16 [16, 2048, 2048], P('section', 'dp')
- projector_grads: bfloat16 [16, 2048, 7168], P('section', None, 'dp')
- layer_losses: float32 [16], P('section')
Inputs may be any that keep to these rules, and one draw needn't show every extreme that they name: Section k holds 4 or 3 teacher layers, three sections the smaller number; boundaries[0] is 0 and boundaries[16] is 61. Teacher layer layer_map[l] lies on a section from l - 2 to l + 2; student layers 0 and 15 pair with layers of sections 1 and 14, student layers 1 and 14 with layers of sections 3 and 12. `valid_counts`: the valid tokens stand first in their micro-batch; the last micro-batch is full.
All inputs are finite; a program needn't handle non-finite values.
Results may differ from a plain program's by a relative error of at most 0.015.
Values may be sent and summed in bfloat16 or wider, within the bound.
A program may use at most 128 MiB of HBM per device.

v0:
```python
import jax
import jax.numpy as jnp
from jax import lax
from jax.sharding import Mesh
from jax.sharding import PartitionSpec as P

DP = ("dp_0", "dp_1")


loss_scale = 128.0
norm_eps = 1e-06


def from_behind(block, axis, distance):
    devices = range(lax.axis_size(axis))
    route = [(i - distance, i) for i in devices if i - distance in devices]
    return lax.ppermute(block, axis, route)


def whole_of(x, axes, dim):
    for axis in reversed(axes):
        x = lax.all_gather(x, axis, axis=dim, tiled=True)
    return x


def copy_for_each(x, axis):
    copies = jnp.broadcast_to(x, (lax.axis_size(axis), *x.shape))
    return lax.all_to_all(copies, axis, split_axis=0, concat_axis=0, tiled=True)


def over_copies(x, axis):
    everything = copy_for_each(x, axis)
    return jnp.sum(everything, axis=0)


def lookup(table, index):
    places = jnp.arange(table.shape[0], dtype=jnp.int32)
    return jnp.sum(jnp.where(places == index, table, 0))


def direct_step(piece, offset):
    return from_behind(piece, "section", offset)


def per_device(student_states, teacher_states, projector, layer_map, boundaries, valid_counts):
    sections = lax.axis_size("section")
    here = lax.axis_index("section")
    held_slots = teacher_states.shape[0]
    inner = boundaries[1:sections]
    owners = jnp.sum((inner[None, :] <= layer_map[:, None]).astype(jnp.int32), axis=1)
    first_layer = lookup(boundaries, here)

    def outgoing(offset):
        destination = here + offset
        inside = (destination >= 0) & (destination < sections)
        wanted = lookup(layer_map, destination)
        owner = lookup(owners, destination)
        place = jnp.clip(wanted - first_layer, 0, held_slots - 1)
        piece = lax.dynamic_index_in_dim(teacher_states, place, 0, keepdims=False)
        return jnp.where(inside & (owner == here), piece, jnp.zeros_like(piece))

    needed = here - lookup(owners, here)
    arrivals = []
    for offset in (-2, -1, 1, 2):
        arrivals.append((offset, direct_step(outgoing(offset), offset)))
    hidden = outgoing(0)
    for offset, arrived in arrivals:
        hidden = jnp.where(needed == offset, arrived, hidden)
    wide = hidden.astype(jnp.float32)
    target = (wide * lax.rsqrt(jnp.mean(wide * wide, axis=1, keepdims=True) + norm_eps)).astype(
        jnp.bfloat16
    )
    columns = lax.all_to_all(target, DP, split_axis=1, concat_axis=0, tiled=True)
    students, counts = (whole_of(student_states[0], DP, 0), whole_of(valid_counts, DP, 0))
    per_batch = student_states.shape[1]
    token_rows = jnp.arange(students.shape[0], dtype=jnp.int32)
    batch_index = token_rows // per_batch
    batches = jnp.arange(counts.shape[0], dtype=jnp.int32)
    limit = jnp.sum(jnp.where(batch_index[:, None] == batches[None, :], counts[None, :], 0), axis=1)
    valid = (token_rows % per_batch < limit).astype(jnp.float32)[:, None]
    total = jnp.sum(counts).astype(jnp.float32)
    weights = projector[0]
    projected = jnp.dot(students, weights, preferred_element_type=jnp.float32)
    residual = projected - columns.astype(jnp.float32)
    squares = jnp.sum(valid * residual * residual)
    teacher_width = weights.shape[1] * lax.axis_size(DP)
    loss = over_copies(squares, DP) / (total * teacher_width)
    scaled = (valid * (loss_scale / total) * residual).astype(jnp.bfloat16)
    student_grad = lax.psum_scatter(
        lax.dot_general(
            scaled, weights, (((1,), (1,)), ((), ())), preferred_element_type=jnp.float32
        ).astype(jnp.bfloat16),
        DP,
        scatter_dimension=0,
        tiled=True,
    )
    projector_grad = lax.dot_general(
        students, scaled, (((0,), (0,)), ((), ())), preferred_element_type=jnp.float32
    ).astype(jnp.bfloat16)
    return (student_grad[None], projector_grad[None], jnp.reshape(loss, (1,)))


def solution(mesh):
    split = Mesh(mesh.devices.reshape(mesh.shape["section"], 4, 4), ("section", "dp_0", "dp_1"))
    return jax.shard_map(
        per_device,
        mesh=split,
        in_specs=(
            P("section", DP, None),
            P("section", DP, None),
            P("section", None, DP),
            P(),
            P(),
            P(DP),
        ),
        out_specs=(P("section", DP, None), P("section", None, DP), P("section")),
        check_vma=False,
    )
```

profile of v0, /device:TPU:6, one launch (start us, length us, event | category | flops | bytes accessed | tf_op | source)
XLA Modules:
  0.0 573.7 jit_solution(18182196803726800490)
XLA Ops:
  7.2 0.0 copy-start
  7.2 0.0 all-gather.5.cloned.1.call-start
  7.2 0.7 all-gather.5.cloned.1.call-update
  7.9 0.0 all-gather.7.cloned.1.call-start
  8.0 0.7 slice.3
  8.7 1.4 fusion.36
  10.1 0.8 convert_reduce_fusion
  10.9 1.5 fusion.26
  19.4 7.4 %constant_dynamic-slice_fusion = (bf16[1,128,7168]{2,1,0:T(8,128)(2,1)}, bf16[1,128,7168]{2,1,0:T(8,128)(2,1)}, bf16[1,128,7168]{2,1,0:T(8,128)(2,1)}, bf16[1,128,7168]{2,1,0:T(8,128)(2,1)}, bf16[1,128,7168]{2,1,0:T(8,128)(2,1)}) fusion(bf16[4,128,7168]{2,1,0:T(8,128)(2,1)} %param.7, s32[]{:T(128)S(6)} %min.20, s32[]{:T(128)S(6)} %min.19, s32[]{:T(128)S(6)} %min.18, ...), kind=kLoop, calls=%fused_computation.42 | loop fusion | bytes 18350100 | tf_op jit(solution)/shard_map/jit(dynamic_index_in_dim)/dynamic_slice | solution.py:59
  26.8 3.9 copy.30
  30.7 1.4 select_bitcast_fusion.3
  32.1 10.4 %collective-permute-start = (bf16[128,7168]{0,1:T(8,128)(2,1)}, bf16[128,7168]{0,1:T(8,128)(2,1)}, u32[]{:S(2)}, u32[]{:S(2)}) collective-permute-start(bf16[128,7168]{0,1:T(8,128)(2,1)} %select_bitcast_fusion.3), channel_id=1, source_target_pairs={{0,32},{16,48},{32,64},{48,80},{64,96},{80,112},{96,128},{112,144}... | collective-permute-start | bytes 5505032 | tf_op jit(solution)/shard_map/ppermute | solution.py:17
  43.2 3.9 copy.31
  47.0 41.4 %all-gather.5.cloned.1.call-done = bf16[1,512,2048]{2,1,0:T(8,128)(2,1)} async-done(((bf16[1,128,2048]{2,1,0:T(8,128)(2,1)}), bf16[1,512,2048]{2,1,0:T(8,128)(2,1)}) %all-gather.5.cloned.1.call-update) | async-done | bytes 2097168 | tf_op jit(solution)/shard_map/all_gather | solution.py:22
  88.4 0.0 all-gather.7.cloned.1.call-update
  88.5 1.4 select_bitcast_fusion.2
  89.8 2.5 collective-permute-start.1
  92.9 3.9 copy.32
  96.8 1.4 select_bitcast_fusion.1
  98.2 1.3 collective-permute-start.2
  100.1 3.9 copy.33
  104.0 1.4 select_bitcast_fusion
  105.4 1.3 collective-permute-start.3
  108.0 3.9 copy.34
  111.9 3.6 collective-permute-done
  115.5 0.0 collective-permute-done.1
  115.5 0.0 collective-permute-done.2
  115.5 127.2 %collective-permute-done.3 = bf16[128,7168]{0,1:T(8,128)(2,1)} collective-permute-done((bf16[128,7168]{0,1:T(8,128)(2,1)}, bf16[128,7168]{0,1:T(8,128)(2,1)}, u32[]{:S(2)}, u32[]{:S(2)}) %collective-permute-start.3) | collective-permute-done | bytes 1835040 | tf_op jit(solution)/shard_map/ppermute | solution.py:17
  242.7 3.3 fusion.4
  246.0 1.6 fusion.5
  247.6 0.0 copy-start.3
  247.6 0.0 copy-start.2
  247.6 63.9 %all-to-all-start = ((bf16[128,16,448]{0,2,1:T(8,128)(2,1)}), bf16[128,16,448]{0,2,1:T(8,128)(2,1)}, u32[]{:S(2)}, u32[]{:S(2)}) async-start(bf16[128,16,448]{0,2,1:T(8,128)(2,1)} %bitcast.52), calls=%async_computation | async-start | bytes 3670016 | tf_op jit(solution)/shard_map/all_to_all | solution.py:73
  311.5 0.0 reduce-scatter.2.cloned.1.call-start
  312.2 0.0 copy-done.3
  312.2 0.6 dynamic-slice
  312.8 0.8 dynamic-update-slice
  313.6 40.3 %all-reduce = s32[4]{0:T(128)S(1)} all-reduce(s32[4]{0:T(128)S(1)} %dynamic-update-slice), channel_id=1, replica_groups=mesh['section'=16,'dp_0'=4,'dp_1'=4] {'dp_1'}, use_global_device_ids=true, to_apply=%add | all-reduce | flops 4 | bytes 32
  353.9 0.0 copy-done.2
  353.9 0.6 dynamic-slice.1
  355.1 0.2 dynamic-update-slice.1
  355.4 7.3 %all-reduce.1 = s32[16]{0:T(128)S(1)} all-reduce(s32[16]{0:T(128)S(1)} %dynamic-update-slice.1), channel_id=1, replica_groups=mesh['section'=16,'dp_0'=4,'dp_1'=4] {'dp_0'}, use_global_device_ids=true, to_apply=%add.1 | all-reduce | flops 16 | bytes 128
  362.7 0.6 reduce_sum.158
  364.0 0.1 select_reduce_fusion
  364.1 0.0 all-to-all-done
  364.1 0.0 all-gather.7.cloned.1.call-done
  364.2 0.0 copy-done
  364.2 8.6 %fusion.6 = (f32[]{:T(128)}, f32[2048,448]{0,1:T(8,128)S(1)}) fusion(f32[2048]{0:T(1024)S(1)} %get-tuple-element.13, bf16[1,2048,448]{1,2,0:T(8,128)(2,1)S(1)} %copy-done, bf16[1,2048,2048]{2,1,0:T(8,128)(2,1)} %all-gather.7.cloned.1.call-done, bf16[128,16,448]{0,2,1:T(8,128)(2,1)} %all-to-all-done), kind=kOutput, calls=%fused_computation.10 | convolution fusion | flops 3762683904 | bytes 15736836 | tf_op jit(solution)/shard_map/dot_general | solution.py:83
  372.8 0.0 copy-start.4
  372.8 1.8 copy-done.4
  374.6 6.8 %convolution_convert_fusion = bf16[2048,2048]{1,0:T(8,128)(2,1)} fusion(bf16[1,2048,448]{1,2,0:T(8,128)(2,1)S(1)} %copy-done, f32[2048,448]{0,1:T(8,128)S(1)} %get-tuple-element.23, f32[2048]{0:T(1024)S(1)} %broadcast_select_fusion), kind=kOutput, calls=%fused_computation.4 | convolution fusion | flops 3764125696 | bytes 13901824 | tf_op jit(solution)/shard_map/dot_general | solution.py:90
  381.4 0.0 reduce-scatter.2.cloned.1.call-update
  381.4 1.2 broadcast_in_dim.52
  382.7 5.7 all-to-all-start.1
  388.4 0.0 copy-start.1
  388.4 9.8 %fusion.12 = bf16[1,2048,448]{1,2,0:T(8,128)(2,1)} fusion(bf16[1,2048,2048]{2,1,0:T(8,128)(2,1)} %all-gather.7.cloned.1.call-done, f32[2048,448]{0,1:T(8,128)} %copy-done.4, f32[2048]{0:T(1024)S(1)} %broadcast_select_fusion), kind=kOutput, calls=%fused_computation.15 | convolution fusion | flops 3760848896 | bytes 13901824 | tf_op jit(solution)/shard_map/dot_general | solution.py:97
  398.2 0.0 all-to-all-done.1
  398.2 0.6 reduce_sum.173
  399.5 166.5 %reduce-scatter.2.cloned.1.call-done = bf16[128,2048]{1,0:T(8,128)(2,1)} async-done(((bf16[2048,2048]{1,0:T(8,128)(2,1)}), bf16[128,2048]{1,0:T(8,128)(2,1)}) %reduce-scatter.2.cloned.1.call-update) | async-done | bytes 524304 | tf_op jit(solution)/shard_map/reduce_scatter | solution.py:89
  566.0 0.0 copy-done.1
  (6 shorter events, 0.0 us)
Async XLA Ops:
  7.2 357.0 %copy-start = (bf16[1,2048,448]{1,2,0:T(8,128)(2,1)S(1)}, bf16[1,2048,448]{1,2,0:T(8,128)(2,1)}, u32[]{:S(2)}) copy-start(bf16[1,2048,448]{1,2,0:T(8,128)(2,1)} %param.8) | copy-start | bytes 5505028
  7.2 81.3 %all-gather.5.cloned.1.call-start = ((), (), s32[]{:S(2)}) async-start(), calls=%async_computation.4 | async-start | bytes 2621440 | tf_op jit(solution)/shard_map/all_gather | solution.py:22
  7.9 356.2 %all-gather.7.cloned.1.call-start = ((), (), s32[]{:S(2)}) async-start(), calls=%async_computation.5 | async-start | bytes 10485760 | tf_op jit(solution)/shard_map/all_gather | solution.py:22
  32.1 83.5 %collective-permute-start = (bf16[128,7168]{0,1:T(8,128)(2,1)}, bf16[128,7168]{0,1:T(8,128)(2,1)}, u32[]{:S(2)}, u32[]{:S(2)}) collective-permute-start(bf16[128,7168]{0,1:T(8,128)(2,1)} %select_bitcast_fusion.3), channel_id=1, source_target_pairs={{0,32},{16,48},{32,64},{48,80},{64,96},{80,112},{96,128},{112,144}... | collective-permute-start | bytes 5505032 | tf_op jit(solution)/shard_map/ppermute | solution.py:17
  89.8 25.7 %collective-permute-start.1 = (bf16[128,7168]{0,1:T(8,128)(2,1)}, bf16[128,7168]{0,1:T(8,128)(2,1)}, u32[]{:S(2)}, u32[]{:S(2)}) collective-permute-start(bf16[128,7168]{0,1:T(8,128)(2,1)} %select_bitcast_fusion.2), channel_id=1, source_target_pairs={{0,16},{16,32},{32,48},{48,64},{64,80},{80,96},{96,112},{112,128},... | collective-permute-start | bytes 5505032 | tf_op jit(solution)/shard_map/ppermute | solution.py:17
  98.2 17.3 %collective-permute-start.2 = (bf16[128,7168]{0,1:T(8,128)(2,1)}, bf16[128,7168]{0,1:T(8,128)(2,1)}, u32[]{:S(2)}, u32[]{:S(2)}) collective-permute-start(bf16[128,7168]{0,1:T(8,128)(2,1)} %select_bitcast_fusion.1), channel_id=1, source_target_pairs={{16,0},{32,16},{48,32},{64,48},{80,64},{96,80},{112,96},{128,112},... | collective-permute-start | bytes 5505032 | tf_op jit(solution)/shard_map/ppermute | solution.py:17
  105.4 137.3 %collective-permute-start.3 = (bf16[128,7168]{0,1:T(8,128)(2,1)}, bf16[128,7168]{0,1:T(8,128)(2,1)}, u32[]{:S(2)}, u32[]{:S(2)}) collective-permute-start(bf16[128,7168]{0,1:T(8,128)(2,1)} %select_bitcast_fusion), channel_id=1, source_target_pairs={{32,0},{48,16},{64,32},{80,48},{96,64},{112,80},{128,96},{144,112}... | collective-permute-start | bytes 5505032 | tf_op jit(solution)/shard_map/ppermute | solution.py:17
  247.6 64.6 %copy-start.3 = (u32[256]{0:T(256)S(1)}, u32[256]{0:T(256)}, u32[]{:S(2)}) copy-start(u32[256]{0:T(256)} %constant.84) | copy-start | bytes 3076
  247.6 106.2 %copy-start.2 = (u32[256]{0:T(256)S(1)}, u32[256]{0:T(256)}, u32[]{:S(2)}) copy-start(u32[256]{0:T(256)} %constant.89) | copy-start | bytes 3076
  247.6 116.5 %all-to-all-start = ((bf16[128,16,448]{0,2,1:T(8,128)(2,1)}), bf16[128,16,448]{0,2,1:T(8,128)(2,1)}, u32[]{:S(2)}, u32[]{:S(2)}) async-start(bf16[128,16,448]{0,2,1:T(8,128)(2,1)} %bitcast.52), calls=%async_computation | async-start | bytes 3670016 | tf_op jit(solution)/shard_map/all_to_all | solution.py:73
  311.5 254.5 %reduce-scatter.2.cloned.1.call-start = ((), (), s32[]{:S(2)}) async-start(), calls=%async_computation.3 | async-start | bytes 8912896 | tf_op jit(solution)/shard_map/reduce_scatter | solution.py:89
  372.8 1.8 copy-start.4
  382.7 15.5 %all-to-all-start.1 = ((f32[16,1,1]{2,1,0:T(1,128)}), f32[16,1,1]{2,1,0:T(1,128)S(1)}, u32[]{:S(2)}, u32[]{:S(2)}) async-start(f32[16,1,1]{2,1,0:T(1,128)} %broadcast_in_dim.52), calls=%async_computation.2 | async-start | bytes 16384 | tf_op jit(solution)/shard_map/all_to_all | solution.py:28
  388.4 177.6 %copy-start.1 = (bf16[1,2048,448]{1,2,0:T(8,128)(2,1)S(1)}, bf16[1,2048,448]{1,2,0:T(8,128)(2,1)}, u32[]{:S(2)}) copy-start(bf16[1,2048,448]{1,2,0:T(8,128)(2,1)} %param.8) | copy-start | bytes 5505028
Sparse Core Ops, SparseCore 0:
  9.8 78.5 all-gather.4
  90.2 244.5 all-gather.6
  381.5 184.4 reduce-scatter.1
where the time goes:
time: 578 us; the launch traced here: 574 us
  waiting for transfers between devices  339 us (59%)
  starting transfers between devices  85.2 us (15%)
  blocking collectives  47.6 us (8%)
  local copies, waits for them, and re-layouts  32.8 us (6%)
  between operations  27.9 us (5%)
  matrix products  25.2 us (4%)
  other arithmetic  15.5 us (3%)
    reduce_scatter x1, waiting for transfers between devices, per_device(): lax.psum_scatter(lax.dot_general(scaled, weights, (((1,), (1,)), ((), ())...  167 us
    ppermute x4, waiting for transfers between devices, from_behind(): return lax.ppermute(block, axis, route)  131 us
    all_to_all x1, starting transfers between devices, per_device(): lax.all_to_all(target, DP, split_axis=1, concat_axis=0, tiled=True)  63.9 us
    unnamed x2, blocking collectives  47.6 us
    all_gather x2, waiting for transfers between devices, whole_of(): x = lax.all_gather(x, axis, axis=dim, tiled=True)  41.4 us
    unnamed x21, local copies, waits for them, and re-layouts  23.4 us
    ppermute x4, starting transfers between devices, from_behind(): return lax.ppermute(block, axis, route)  15.5 us
  transfers between devices with their start and end apart: 9, of which 4 were waited for; matrix products, arithmetic and copies ran while one was open for 10% of the time, Pallas kernels for 0%

commit v1 on v0

v1 whole, which is shorter than its diff:
```python
import functools

import jax
import jax.numpy as jnp
from jax import lax
from jax.experimental import pallas as pl
from jax.experimental.pallas import tpu as pltpu
from jax.sharding import Mesh
from jax.sharding import PartitionSpec as P

F32 = jnp.float32
BF16 = jnp.bfloat16
MESH = pl.DeviceIdType.MESH
loss_scale = 128.0
norm_eps = 1e-06
N = 4


def kernel(
    lm,
    bd,
    vc,
    x_hbm,
    t_hbm,
    w_hbm,
    gown,
    zrecv,
    pown,
    precv,
    loss,
    tv,
    blk,
    snd,
    rcv,
    yrcv,
    xall,
    wpair,
    tl,
    tc,
    sall,
    grads,
    xrecv,
    zsend,
    psend,
    cnt,
    lsum,
    sq,
    loc_sem,
    x_ss,
    x_rs,
    w_ss,
    w_rs,
    c_ss,
    c_rs,
    d_ss,
    d_rs,
    y_ss,
    y_rs,
    l_ss,
    l_rs,
    k_ss,
    k_rs,
    gx_ss,
    gx_rs,
    gz_ss,
    gz_rs,
    p_ss,
    p_rs,
    q_ss,
    q_rs,
):
    y, zh, c = lax.axis_index("y"), lax.axis_index("zh"), lax.axis_index("c")
    x, zl = lax.axis_index("x"), lax.axis_index("zl")
    here = y * 4 + zh * 2 + c
    me = x * N + zl
    xp = 3 - x
    half, pair = lax.rem(x, 2), lax.div(x, 2)
    wp = x + 1 - 2 * half
    y_to = lax.rem(y + 2 * zh - 1 + 4, 4)
    y_from = lax.rem(y - 2 * zh + 1 + 4, 4)
    tokens = x_hbm.shape[1]
    width = w_hbm.shape[2]
    rest = DT_GROUPS * width

    def z_at(k):
        return lax.rem(zl + k, N)

    def z_back(k):
        return lax.rem(zl + N - k, N)

    def send(src, dst, ss, rs, where):
        copy = pltpu.make_async_remote_copy(
            src_ref=src, dst_ref=dst, send_sem=ss, recv_sem=rs, device_id=where, device_id_type=MESH
        )
        copy.start()
        return copy

    def arrived(dst, ss, rs):
        pltpu.make_async_remote_copy(
            src_ref=dst,
            dst_ref=dst,
            send_sem=ss,
            recv_sem=rs,
            device_id={"c": 1 - c},
            device_id_type=MESH,
        ).wait_recv()

    sent = []
    t_copy = pltpu.make_async_copy(t_hbm, tv, loc_sem.at[0])
    t_copy.start()
    x_copy = pltpu.make_async_copy(x_hbm.at[0], xall.at[zl], loc_sem.at[1])
    x_copy.start()
    w_copy = pltpu.make_async_copy(w_hbm.at[0], wpair.at[half], loc_sem.at[2])
    w_copy.start()
    cnt[me] = jnp.full(cnt.shape[1:], vc[0], jnp.int32)

    others = [(kx, kz) for kx in range(N) for kz in range(N) if (kx, kz) != (0, 0)]
    barrier = pltpu.get_barrier_semaphore()
    greeted = [{"c": 1 - c}, {"y": y_to}, {"y": y_from}]
    greeted += [{"x": lax.rem(x + kx, N), "zl": z_at(kz)} for kx, kz in others]
    greeted += [{"zh": 1 - zh, "x": px, "zl": z_at(kz)} for px in (x, xp) for kz in range(N)]
    for where in greeted:
        pl.semaphore_signal(barrier, inc=1, device_id=where, device_id_type=MESH)
    pl.semaphore_wait(barrier, len(greeted))

    for k in (2, 1, 3):
        sent.append(
            send(x_hbm.at[0], xall.at[zl], x_ss.at[k], x_rs.at[zl], {"zl": z_at(k)})
        )
    sent.append(send(x_hbm.at[0], xall.at[N + zl], x_ss.at[0], x_rs.at[N + zl], {"x": xp}))
    sent.append(send(w_hbm.at[0], wpair.at[half], w_ss, w_rs, {"x": wp}))
    for n, (kx, kz) in enumerate(others):
        where = {"x": lax.rem(x + kx, N), "zl": z_at(kz)}
        sent.append(send(cnt.at[me], cnt.at[me], c_ss.at[n], c_rs.at[me], where))

    def plan(offset):
        to = here + offset
        inside = (to >= 0) & (to < 16)
        layer = lm[jnp.clip(to, 0, 15)]
        owner = jnp.int32(0)
        for k in range(1, 16):
            owner = owner + jnp.where(bd[k] <= layer, 1, 0)
        place = jnp.clip(layer - bd[here], 0, tv.shape[0] - 1)
        return place, jnp.where(inside & (owner == here), F32(1.0), F32(0.0))

    def normalize(offset, dst):
        place, keep = plan(offset)

        def rows16(r, carry):
            rows = pl.ds(pl.multiple_of(r * 16, 16), 16)
            h = tv[place, rows, :].astype(F32)
            scale = lax.rsqrt(jnp.mean(h * h, axis=1, keepdims=True) + norm_eps) * keep
            out = (h * scale).astype(BF16)
            for p in range(2):
                for z in range(N):
                    for e in range(2):
                        at = width * (8 * p + 4 * e + z)
                        dst[p * N + z, rows, e * width : (e + 1) * width] = out[:, at : at + width]
            return carry

        lax.fori_loop(0, tokens // 16, rows16, 0)

    def chunk(q, z):
        return (pair + q - 2 * pair * q) * N + z

    def merge(dst, other):
        def rows16(r, carry):
            rows = pl.ds(pl.multiple_of(r * 16, 16), 16)
            dst[rows, :] = dst[rows, :] + other[rows, :]
            return carry

        lax.fori_loop(0, tokens // 16, rows16, 0)

    t_copy.wait()
    for n, offset in enumerate((-1, 1)):
        normalize(offset, snd.at[n])
        sent.append(send(snd.at[n], rcv.at[n], d_ss.at[n], d_rs.at[n], {"c": 1 - c}))
    normalize(-2, blk.at[0])
    normalize(2, blk.at[2])
    arrived(rcv.at[1 - c], d_ss.at[1 - c], d_rs.at[1 - c])

    def merge_far(i, carry):
        merge(blk.at[2 * (1 - c), i], rcv.at[1 - c, i])
        return carry

    lax.fori_loop(0, 2 * N, merge_far, 0)
    order = [(q, k) for q in (1, 0) for k in (2, 1, 3, 0)]
    for q, k in order:
        i = chunk(q, z_at(k))
        sent.append(
            send(blk.at[2 * zh, i], yrcv.at[i], y_ss.at[i], y_rs.at[i], {"y": y_to})
        )
    normalize(0, blk.at[1])
    arrived(rcv.at[c], d_ss.at[c], d_rs.at[c])

    def merge_near(i, carry):
        merge(blk.at[1, i], rcv.at[c, i])
        return carry

    lax.fori_loop(0, 2 * N, merge_near, 0)
    for q, k in order:
        i = chunk(q, z_at(k))
        slot = q * N + zl
        if (q, k) == (0, 0):
            own = pltpu.make_async_copy(blk.at[1, i], tl.at[slot], loc_sem.at[3])
            own.start()
        else:
            where = {"x": xp, "zl": z_at(k)} if q else {"zl": z_at(k)}
            sent.append(send(blk.at[1, i], tl.at[slot], l_ss.at[q * N + k], l_rs.at[slot], where))

    for k in (2, 1, 3):
        z = z_back(k)
        arrived(xall.at[z], x_ss.at[k], x_rs.at[z])
        sent.append(send(xall.at[z], xall.at[N + z], x_ss.at[N + k], x_rs.at[N + z], {"x": xp}))

    for q, k in order:
        i = chunk(q, z_at(k))
        arrived(yrcv.at[i], y_ss.at[i], y_rs.at[i])
        merge(blk.at[2 * (1 - zh), i], yrcv.at[i])
        where = {"zh": 1 - zh, "x": xp if q else x, "zl": z_at(k)}
        sent.append(
            send(
                blk.at[2 * (1 - zh), i],
                tc.at[q * N + zl],
                k_ss.at[q * N + k],
                k_rs.at[q * N + zl],
                where,
            )
        )

    for n, (kx, kz) in enumerate(others):
        d = lax.rem(x + kx, N) * N + z_at(kz)
        arrived(cnt.at[d], c_ss.at[n], c_rs.at[d])
    total = cnt[0, 0:1, 0:1]
    for d in range(1, N * N):
        total = total + cnt[d, 0:1, 0:1]
    total = total.astype(F32)
    factor = loss_scale / total
    x_copy.wait()
    w_copy.wait()
    arrived(wpair.at[1 - half], w_ss, w_rs)
    own.wait()
    sq[...] = jnp.zeros_like(sq)

    def token_block(q, z):
        slot = q * N + z
        d = (xp if q else x) * N + z
        row = lax.broadcasted_iota(jnp.int32, (tokens, width), 0)
        valid = jnp.where(row < cnt[d, 0:1, 0:1], F32(1.0), F32(0.0))
        base = pl.multiple_of(slot * tokens, tokens)
        for e in range(2):
            at = slice(e * width, (e + 1) * width)
            target = tl[slot, :, at].astype(F32) + tc[slot, :, at].astype(F32)
            got = jnp.dot(xall[slot], wpair[e], preferred_element_type=F32)
            residual = got - target
            masked = valid * residual
            sq[...] += jnp.sum(masked * residual, axis=0, keepdims=True)
            sall[e, pl.ds(base, tokens), :] = (masked * factor).astype(BF16)
        nt = (((1,), (1,)), ((), ()))
        for m in range(4):
            cols = slice(m * 512, (m + 1) * 512)
            part = lax.dot_general(
                sall[0, pl.ds(base, tokens), :], wpair[0, cols, :], nt, preferred_element_type=F32
            )
            part += lax.dot_general(
                sall[1, pl.ds(base, tokens), :], wpair[1, cols, :], nt, preferred_element_type=F32
            )
            grads[slot, :, cols] = part.astype(BF16)

    def far_block(k, carry):
        z = lax.rem(zl + N - k, N)
        slot = N + z
        arrived(xall.at[slot], x_ss.at[k], x_rs.at[slot])
        arrived(tl.at[slot], l_ss.at[slot], l_rs.at[slot])
        arrived(tc.at[slot], k_ss.at[slot], k_rs.at[slot])
        token_block(1, z)
        send(grads.at[slot], xrecv.at[z], gx_ss.at[z], gx_rs.at[z], {"x": xp})
        return carry

    def near_block(k, carry):
        z = lax.rem(zl + N - k, N)

        @pl.when(k > 0)
        def _():
            arrived(tl.at[z], l_ss.at[z], l_rs.at[z])

        arrived(tc.at[z], k_ss.at[z], k_rs.at[z])
        token_block(0, z)
        return carry

    lax.fori_loop(0, N, far_block, 0)
    lax.fori_loop(0, N, near_block, 0)

    lsum[me] = jnp.full(lsum.shape[1:], jnp.sum(sq[...]), F32)
    for n, (kx, kz) in enumerate(others):
        where = {"x": lax.rem(x + kx, N), "zl": z_at(kz)}
        sent.append(send(lsum.at[me], lsum.at[me], q_ss.at[n], q_rs.at[me], where))

    students = 2048
    step = 256

    def project(e, dst):
        def columns(j, carry):
            cols = pl.ds(pl.multiple_of(j * step, step), step)
            total_part = jnp.zeros((step, width), F32)
            for b in range(2 * N):
                total_part += lax.dot_general(
                    xall[b, :, cols],
                    sall[e, b * tokens : (b + 1) * tokens, :],
                    (((0,), (0,)), ((), ())),
                    preferred_element_type=F32,
                )
            dst[cols, :] = total_part.astype(dst.dtype)
            return carry

        lax.fori_loop(0, students // step, columns, 0)

    project(1 - half, psend)
    sent.append(send(psend, precv, p_ss, p_rs, {"x": wp}))

    def summed(z, dst):
        def rows16(r, carry):
            rows = pl.ds(pl.multiple_of(r * 16, 16), 16)
            both = grads[z, rows, :].astype(F32) + xrecv[z, rows, :].astype(F32)
            dst[rows, :] = both.astype(dst.dtype)
            return carry

        arrived(xrecv.at[z], gx_ss.at[z], gx_rs.at[z])
        lax.fori_loop(0, tokens // 16, rows16, 0)

    for k in (1, 2, 3):
        z = z_back(k)
        summed(z, zsend.at[k - 1])
        sent.append(
            send(zsend.at[k - 1], zrecv.at[N - 1 - k], gz_ss.at[k - 1], gz_rs.at[N - 1 - k], {"zl": z})
        )
    project(half, pown)
    summed(zl, gown)

    for n, (kx, kz) in enumerate(others):
        d = lax.rem(x + kx, N) * N + z_at(kz)
        arrived(lsum.at[d], q_ss.at[n], q_rs.at[d])
    squares = lsum[0]
    for d in range(1, N * N):
        squares = squares + lsum[d]
    loss[...] = squares / (total * rest)

    for k in range(3):
        arrived(zrecv.at[k], gz_ss.at[k], gz_rs.at[k])
    arrived(precv, p_ss, p_rs)

    def far_sent(z, carry):
        pltpu.make_async_remote_copy(
            src_ref=grads.at[N + z],
            dst_ref=xrecv.at[z],
            send_sem=gx_ss.at[z],
            recv_sem=gx_rs.at[z],
            device_id={"x": xp},
            device_id_type=MESH,
        ).wait_send()
        return carry

    lax.fori_loop(0, N, far_sent, 0)
    for copy in sent:
        copy.wait_send()


DT_GROUPS = 16


def per_device(student_states, teacher_states, projector, layer_map, boundaries, valid_counts):
    slots, tokens, features = teacher_states.shape
    students = student_states.shape[2]
    width = projector.shape[2]
    any_space = pl.BlockSpec(memory_space=pl.ANY)
    smem = pl.BlockSpec(memory_space=pltpu.SMEM)
    vmem = pl.BlockSpec(memory_space=pltpu.VMEM)
    dma = pltpu.SemaphoreType.DMA
    piece = (2 * N, tokens, 2 * width)
    gown, zrecv, pown, precv, loss = pl.pallas_call(
        kernel,
        out_shape=(
            jax.ShapeDtypeStruct((tokens, students), F32),
            jax.ShapeDtypeStruct((3, tokens, students), BF16),
            jax.ShapeDtypeStruct((students, width), F32),
            jax.ShapeDtypeStruct((students, width), BF16),
            jax.ShapeDtypeStruct((8, 128), F32),
        ),
        in_specs=[smem, smem, smem, any_space, any_space, any_space],
        out_specs=(vmem, any_space, vmem, any_space, vmem),
        scratch_shapes=[
            pltpu.VMEM((slots, tokens, features), BF16),
            pltpu.VMEM((3, *piece), BF16),
            pltpu.VMEM((2, *piece), BF16),
            pltpu.VMEM((2, *piece), BF16),
            pltpu.VMEM(piece, BF16),
            pltpu.VMEM((2 * N, tokens, students), BF16),
            pltpu.VMEM((2, students, width), BF16),
            pltpu.VMEM(piece, BF16),
            pltpu.VMEM(piece, BF16),
            pltpu.VMEM((2, 2 * N * tokens, width), BF16),
            pltpu.VMEM((2 * N, tokens, students), BF16),
            pltpu.VMEM((N, tokens, students), BF16),
            pltpu.VMEM((3, tokens, students), BF16),
            pltpu.VMEM((students, width), BF16),
            pltpu.VMEM((N * N, 8, 128), jnp.int32),
            pltpu.VMEM((N * N, 8, 128), F32),
            pltpu.VMEM((1, width), F32),
            dma((4,)),
            dma((2 * N,)),
            dma((2 * N,)),
            dma,
            dma,
            dma((16,)),
            dma((16,)),
            dma((2,)),
            dma((2,)),
            dma((2 * N,)),
            dma((2 * N,)),
            dma((2 * N,)),
            dma((2 * N,)),
            dma((2 * N,)),
            dma((2 * N,)),
            dma((N,)),
            dma((N,)),
            dma((3,)),
            dma((3,)),
            dma,
            dma,
            dma((16,)),
            dma((16,)),
        ],
        compiler_params=pltpu.CompilerParams(
            collective_id=0, has_side_effects=True, vmem_limit_bytes=67043328
        ),
    )(layer_map, boundaries, valid_counts, student_states, teacher_states, projector)
    student_grad = gown
    for k in range(3):
        student_grad = student_grad + zrecv[k].astype(F32)
    projector_grad = pown + precv.astype(F32)
    return student_grad.astype(BF16)[None], projector_grad.astype(BF16)[None], loss[0, 0:1]


def solution(mesh):
    axes = ("y", "zh", "c", "x", "zl")
    split = Mesh(mesh.devices.reshape(4, 2, 2, N, N), axes)
    section, dp = axes[:3], axes[3:]
    return jax.shard_map(
        per_device,
        mesh=split,
        in_specs=(P(section, dp, None), P(section, dp, None), P(section, None, dp), P(), P(), P(dp)),
        out_specs=(P(section, dp, None), P(section, None, dp), P(section)),
        check_vma=False,
    )
```

time: 578 us -> 219 us (0.38)
  waiting for transfers between devices: 339 us -> 0 us
  Pallas kernels: 0 us -> 204 us
  starting transfers between devices: 85.2 us -> 0 us
  blocking collectives: 47.6 us -> 0 us
  between operations: 27.9 us -> 1.3 us
  local copies, waits for them, and re-layouts: 32.8 us -> 7.46 us
  matrix products: 25.2 us -> 0 us
  other arithmetic: 15.5 us -> 5.8 us
    pallas_call x0 -> x1, Pallas kernels: none -> 204 us  [per_device(): pl.pallas_call(kernel, out_shape=(jax.ShapeDtypeStruct((tokens, students)...]
    reduce_scatter x1 -> x0, waiting for transfers between devices: 167 us -> none  [per_device(): lax.psum_scatter(lax.dot_general(scaled, weights, (((1,), (1,)), ((), ())...]
    ppermute x4 -> x0, waiting for transfers between devices: 131 us -> none  [from_behind(): return lax.ppermute(block, axis, route)]
    all_to_all x2 -> x0, starting transfers between devices: 69.6 us -> none  [the longest x1 63.9 us: per_device(): lax.all_to_all(target, DP, split_axis=1, concat_axis=0, tiled=True)]
    unnamed x2 -> x0, blocking collectives: 47.6 us -> none
    all_gather x2 -> x0, waiting for transfers between devices: 41.4 us -> none  [whole_of(): x = lax.all_gather(x, axis, axis=dim, tiled=True)]
    dot_general x3 -> x0, matrix products: 25.2 us -> none  [the longest x1 9.8 us: per_device(): lax.dot_general(students, scaled, (((0,), (0,)), ((), ())), preferred_ele...]
    unnamed x21 -> x4, local copies, waits for them, and re-layouts: 23.4 us -> 6.12 us
  transfers between devices with their start and end apart: 9 -> 0, of which waited for: 4 -> 0; matrix products, arithmetic and copies ran while one was open for 10% -> 0% of each run, Pallas kernels for 0% -> 0%
where the time goes in v1:
time: 219 us
  Pallas kernels  204 us (93%)
  local copies, waits for them, and re-layouts  7.46 us (3%)
  other arithmetic  5.8 us (3%)
    pallas_call x1, Pallas kernels, per_device(): pl.pallas_call(kernel, out_shape=(jax.ShapeDtypeStruct((tokens, students)...  204 us
    unnamed x4, local copies, waits for them, and re-layouts  6.12 us

profile of v1, /device:TPU:6, one launch (start us, length us, event | category | flops | bytes accessed | tf_op | source)
XLA Modules:
  0.0 219.0 jit_solution(15258495856193054976)
XLA Ops:
  1.3 3.8 %copy.9.w_hbm = bf16[1,2048,448]{2,1,0:T(8,128)(2,1)} copy(bf16[1,2048,448]{1,2,0:T(8,128)(2,1)} %param.8) | data formatting | bytes 3670016 | tf_op args[2]
  5.1 204.4 %shard_map.85 = (f32[128,2048]{1,0:T(8,128)}, bf16[3,128,2048]{2,1,0:T(8,128)(2,1)}, f32[2048,448]{1,0:T(8,128)}, bf16[2048,448]{1,0:T(8,128)(2,1)}, f32[8,128]{1,0:T(8,128)}) custom-call(s32[16]{0:T(128)} %lm.1, s32[17]{0:T(128)} %bd.1, s32[1]{0:T(128)S(6)} %copy.11.vc, bf16[1,128,2048]{2,1,0:T(8,128)(2,1)} %x_hbm.1, bf16[4,128,7168]{2,1,0:T(8,128)(2,1)} %t_hbm.1, ...), custom_call_target="tpu_custom_call" | custom-call | tf_op jit(solution)/shard_map/pallas_call | solution.py:380
  209.5 0.0 copy-start
  209.5 1.3 slice.15
  210.9 2.8 %fusion.2 = bf16[1,128,2048]{2,1,0:T(8,128)(2,1)} fusion(f32[128,2048]{1,0:T(8,128)} %get-tuple-element.8, bf16[3,128,2048]{2,1,0:T(8,128)(2,1)} %get-tuple-element.9), kind=kLoop, calls=%fused_computation.6 | loop fusion | flops 1835008 | bytes 3145728 | tf_op jit(solution)/shard_map/broadcast_in_dim | solution.py:441
  213.6 0.0 copy-done
  213.6 3.1 %fusion = bf16[1,2048,448]{2,1,0:T(8,128)(2,1)S(1)} fusion(f32[2048,448]{1,0:T(8,128)} %get-tuple-element.10, bf16[2048,448]{1,0:T(8,128)(2,1)S(1)} %copy-done), kind=kLoop, calls=%fused_computation.1 | loop fusion | flops 2752512 | bytes 7340032 | tf_op jit(solution)/shard_map/broadcast_in_dim | solution.py:441
  216.7 2.3 %copy.10 = bf16[1,2048,448]{1,2,0:T(8,128)(2,1)} copy(bf16[1,2048,448]{2,1,0:T(8,128)(2,1)S(1)} %fusion) | data formatting | bytes 3670016
Async XLA Ops:
  209.5 4.1 %copy-start = (bf16[2048,448]{1,0:T(8,128)(2,1)S(1)}, bf16[2048,448]{1,0:T(8,128)(2,1)}, u32[]{:S(2)}) copy-start(bf16[2048,448]{1,0:T(8,128)(2,1)} %get-tuple-element.11) | copy-start | bytes 5505028

commit v2 on v1

--- a/solution.py
+++ b/solution.py
@@ -23,8 +23,7 @@
     x_hbm,
     t_hbm,
     w_hbm,
-    gown,
-    zrecv,
+    gout,
     pown,
     precv,
     loss,
@@ -41,12 +40,16 @@
     grads,
     xrecv,
     zsend,
+    zrecv,
+    gown,
     psend,
     cnt,
     lsum,
     sq,
     loc_sem,
-    x_ss,
+    xr_ss,
+    xl_ss,
+    xx_ss,
     x_rs,
     w_ss,
     w_rs,
@@ -79,7 +82,8 @@
     y_to = lax.rem(y + 2 * zh - 1 + 4, 4)
     y_from = lax.rem(y - 2 * zh + 1 + 4, 4)
     tokens = x_hbm.shape[1]
-    width = w_hbm.shape[2]
+    width = w_hbm.shape[1]
+    students = w_hbm.shape[2]
     rest = DT_GROUPS * width
 
     def z_at(k):
@@ -123,11 +127,50 @@
         pl.semaphore_signal(barrier, inc=1, device_id=where, device_id_type=MESH)
     pl.semaphore_wait(barrier, len(greeted))
 
-    for k in (2, 1, 3):
-        sent.append(
-            send(x_hbm.at[0], xall.at[zl], x_ss.at[k], x_rs.at[zl], {"zl": z_at(k)})
-        )
-    sent.append(send(x_hbm.at[0], xall.at[N + zl], x_ss.at[0], x_rs.at[N + zl], {"x": xp}))
+    def right(b, act):
+        @pl.when(zl < N - 1)
+        def _():
+            act(x_block(b), xall.at[b], xr_ss.at[b], x_rs.at[b], {"zl": zl + 1})
+
+    def left(b, act):
+        @pl.when(zl > 0)
+        def _():
+            act(x_block(b), xall.at[b], xl_ss.at[b], x_rs.at[b], {"zl": zl - 1})
+
+    def across(b, act):
+        act(x_block(b), xall.at[N + b], xx_ss.at[b], x_rs.at[N + b], {"x": xp})
+
+    def x_block(b):
+        return x_hbm.at[0] if b is zl else xall.at[b]
+
+    def from_left(j, act):
+        @pl.when(zl - j >= 0)
+        def _():
+            right(zl - j, act)
+            across(zl - j, act)
+
+    def from_right(j, act):
+        @pl.when(zl + j < N)
+        def _():
+            left(zl + j, act)
+            across(zl + j, act)
+
+    def forward(j):
+        @pl.when(zl - j >= 0)
+        def _():
+            arrived(xall.at[zl - j], xx_ss.at[zl - j], x_rs.at[zl - j])
+
+        from_left(j, send)
+
+        @pl.when(zl + j < N)
+        def _():
+            arrived(xall.at[zl + j], xx_ss.at[zl + j], x_rs.at[zl + j])
+
+        from_right(j, send)
+
+    right(zl, send)
+    left(zl, send)
+    across(zl, send)
     sent.append(send(w_hbm.at[0], wpair.at[half], w_ss, w_rs, {"x": wp}))
     for n, (kx, kz) in enumerate(others):
         where = {"x": lax.rem(x + kx, N), "zl": z_at(kz)}
@@ -175,6 +218,7 @@
     for n, offset in enumerate((-1, 1)):
         normalize(offset, snd.at[n])
         sent.append(send(snd.at[n], rcv.at[n], d_ss.at[n], d_rs.at[n], {"c": 1 - c}))
+    forward(1)
     normalize(-2, blk.at[0])
     normalize(2, blk.at[2])
     arrived(rcv.at[1 - c], d_ss.at[1 - c], d_rs.at[1 - c])
@@ -184,7 +228,7 @@
         return carry
 
     lax.fori_loop(0, 2 * N, merge_far, 0)
-    order = [(q, k) for q in (1, 0) for k in (2, 1, 3, 0)]
+    order = [(q, k) for q in (1, 0) for k in (1, 2, 3, 0)]
     for q, k in order:
         i = chunk(q, z_at(k))
         sent.append(
@@ -208,10 +252,7 @@
             where = {"x": xp, "zl": z_at(k)} if q else {"zl": z_at(k)}
             sent.append(send(blk.at[1, i], tl.at[slot], l_ss.at[q * N + k], l_rs.at[slot], where))
 
-    for k in (2, 1, 3):
-        z = z_back(k)
-        arrived(xall.at[z], x_ss.at[k], x_rs.at[z])
-        sent.append(send(xall.at[z], xall.at[N + z], x_ss.at[N + k], x_rs.at[N + z], {"x": xp}))
+    forward(2)
 
     for q, k in order:
         i = chunk(q, z_at(k))
@@ -228,6 +269,8 @@
             )
         )
 
+    forward(3)
+
     for n, (kx, kz) in enumerate(others):
         d = lax.rem(x + kx, N) * N + z_at(kz)
         arrived(cnt.at[d], c_ss.at[n], c_rs.at[d])
@@ -248,29 +291,29 @@
         row = lax.broadcasted_iota(jnp.int32, (tokens, width), 0)
         valid = jnp.where(row < cnt[d, 0:1, 0:1], F32(1.0), F32(0.0))
         base = pl.multiple_of(slot * tokens, tokens)
+        nt = (((1,), (1,)), ((), ()))
         for e in range(2):
             at = slice(e * width, (e + 1) * width)
             target = tl[slot, :, at].astype(F32) + tc[slot, :, at].astype(F32)
-            got = jnp.dot(xall[slot], wpair[e], preferred_element_type=F32)
+            got = lax.dot_general(xall[slot], wpair[e], nt, preferred_element_type=F32)
             residual = got - target
             masked = valid * residual
             sq[...] += jnp.sum(masked * residual, axis=0, keepdims=True)
             sall[e, pl.ds(base, tokens), :] = (masked * factor).astype(BF16)
-        nt = (((1,), (1,)), ((), ()))
         for m in range(4):
             cols = slice(m * 512, (m + 1) * 512)
-            part = lax.dot_general(
-                sall[0, pl.ds(base, tokens), :], wpair[0, cols, :], nt, preferred_element_type=F32
+            part = jnp.dot(
+                sall[0, pl.ds(base, tokens), :], wpair[0, :, cols], preferred_element_type=F32
             )
-            part += lax.dot_general(
-                sall[1, pl.ds(base, tokens), :], wpair[1, cols, :], nt, preferred_element_type=F32
+            part += jnp.dot(
+                sall[1, pl.ds(base, tokens), :], wpair[1, :, cols], preferred_element_type=F32
             )
             grads[slot, :, cols] = part.astype(BF16)
 
     def far_block(k, carry):
-        z = lax.rem(zl + N - k, N)
+        z = lax.rem(zl + N - k - 1, N)
         slot = N + z
-        arrived(xall.at[slot], x_ss.at[k], x_rs.at[slot])
+        arrived(xall.at[slot], xx_ss.at[z], x_rs.at[slot])
         arrived(tl.at[slot], l_ss.at[slot], l_rs.at[slot])
         arrived(tc.at[slot], k_ss.at[slot], k_rs.at[slot])
         token_block(1, z)
@@ -278,9 +321,9 @@
         return carry
 
     def near_block(k, carry):
-        z = lax.rem(zl + N - k, N)
-
-        @pl.when(k > 0)
+        z = lax.rem(zl + N - k - 1, N)
+
+        @pl.when(k < N - 1)
         def _():
             arrived(tl.at[z], l_ss.at[z], l_rs.at[z])
 
@@ -296,21 +339,16 @@
         where = {"x": lax.rem(x + kx, N), "zl": z_at(kz)}
         sent.append(send(lsum.at[me], lsum.at[me], q_ss.at[n], q_rs.at[me], where))
 
-    students = 2048
     step = 256
 
     def project(e, dst):
         def columns(j, carry):
             cols = pl.ds(pl.multiple_of(j * step, step), step)
-            total_part = jnp.zeros((step, width), F32)
-            for b in range(2 * N):
-                total_part += lax.dot_general(
-                    xall[b, :, cols],
-                    sall[e, b * tokens : (b + 1) * tokens, :],
-                    (((0,), (0,)), ((), ())),
-                    preferred_element_type=F32,
-                )
-            dst[cols, :] = total_part.astype(dst.dtype)
+            block = xall[:, :, cols].reshape(2 * N * tokens, step)
+            total_part = lax.dot_general(
+                sall[e], block, (((0,), (0,)), ((), ())), preferred_element_type=F32
+            )
+            dst[:, cols] = total_part.astype(dst.dtype)
             return carry
 
         lax.fori_loop(0, students // step, columns, 0)
@@ -347,17 +385,32 @@
 
     for k in range(3):
         arrived(zrecv.at[k], gz_ss.at[k], gz_rs.at[k])
+
+    def result(r, carry):
+        rows = pl.ds(pl.multiple_of(r * 16, 16), 16)
+        value = gown[rows, :]
+        for k in range(3):
+            value = value + zrecv[k, rows, :].astype(F32)
+        gout[rows, :] = value.astype(BF16)
+        return carry
+
+    lax.fori_loop(0, tokens // 16, result, 0)
     arrived(precv, p_ss, p_rs)
 
+    def drain(src, dst, ss, rs, where):
+        pltpu.make_async_remote_copy(
+            src_ref=src, dst_ref=dst, send_sem=ss, recv_sem=rs, device_id=where, device_id_type=MESH
+        ).wait_send()
+
+    right(zl, drain)
+    left(zl, drain)
+    across(zl, drain)
+    for j in (1, 2, 3):
+        from_left(j, drain)
+        from_right(j, drain)
+
     def far_sent(z, carry):
-        pltpu.make_async_remote_copy(
-            src_ref=grads.at[N + z],
-            dst_ref=xrecv.at[z],
-            send_sem=gx_ss.at[z],
-            recv_sem=gx_rs.at[z],
-            device_id={"x": xp},
-            device_id_type=MESH,
-        ).wait_send()
+        drain(grads.at[N + z], xrecv.at[z], gx_ss.at[z], gx_rs.at[z], {"x": xp})
         return carry
 
     lax.fori_loop(0, N, far_sent, 0)
@@ -371,23 +424,23 @@
 def per_device(student_states, teacher_states, projector, layer_map, boundaries, valid_counts):
     slots, tokens, features = teacher_states.shape
     students = student_states.shape[2]
-    width = projector.shape[2]
+    weights = jnp.swapaxes(projector, 1, 2)
+    width = weights.shape[1]
     any_space = pl.BlockSpec(memory_space=pl.ANY)
     smem = pl.BlockSpec(memory_space=pltpu.SMEM)
     vmem = pl.BlockSpec(memory_space=pltpu.VMEM)
     dma = pltpu.SemaphoreType.DMA
     piece = (2 * N, tokens, 2 * width)
-    gown, zrecv, pown, precv, loss = pl.pallas_call(
+    gout, pown, precv, loss = pl.pallas_call(
         kernel,
         out_shape=(
-            jax.ShapeDtypeStruct((tokens, students), F32),
-            jax.ShapeDtypeStruct((3, tokens, students), BF16),
-            jax.ShapeDtypeStruct((students, width), F32),
-            jax.ShapeDtypeStruct((students, width), BF16),
+            jax.ShapeDtypeStruct((tokens, students), BF16),
+            jax.ShapeDtypeStruct((width, students), F32),
+            jax.ShapeDtypeStruct((width, students), BF16),
             jax.ShapeDtypeStruct((8, 128), F32),
         ),
         in_specs=[smem, smem, smem, any_space, any_space, any_space],
-        out_specs=(vmem, any_space, vmem, any_space, vmem),
+        out_specs=(vmem, vmem, any_space, vmem),
         scratch_shapes=[
             pltpu.VMEM((slots, tokens, features), BF16),
             pltpu.VMEM((3, *piece), BF16),
@@ -395,19 +448,23 @@
             pltpu.VMEM((2, *piece), BF16),
             pltpu.VMEM(piece, BF16),
             pltpu.VMEM((2 * N, tokens, students), BF16),
-            pltpu.VMEM((2, students, width), BF16),
+            pltpu.VMEM((2, width, students), BF16),
             pltpu.VMEM(piece, BF16),
             pltpu.VMEM(piece, BF16),
             pltpu.VMEM((2, 2 * N * tokens, width), BF16),
             pltpu.VMEM((2 * N, tokens, students), BF16),
             pltpu.VMEM((N, tokens, students), BF16),
             pltpu.VMEM((3, tokens, students), BF16),
-            pltpu.VMEM((students, width), BF16),
+            pltpu.VMEM((3, tokens, students), BF16),
+            pltpu.VMEM((tokens, students), F32),
+            pltpu.VMEM((width, students), BF16),
             pltpu.VMEM((N * N, 8, 128), jnp.int32),
             pltpu.VMEM((N * N, 8, 128), F32),
             pltpu.VMEM((1, width), F32),
             dma((4,)),
-            dma((2 * N,)),
+            dma((N,)),
+            dma((N,)),
+            dma((N,)),
             dma((2 * N,)),
             dma,
             dma,
@@ -433,12 +490,9 @@
         compiler_params=pltpu.CompilerParams(
             collective_id=0, has_side_effects=True, vmem_limit_bytes=67043328
         ),
-    )(layer_map, boundaries, valid_counts, student_states, teacher_states, projector)
-    student_grad = gown
-    for k in range(3):
-        student_grad = student_grad + zrecv[k].astype(F32)
-    projector_grad = pown + precv.astype(F32)
-    return student_grad.astype(BF16)[None], projector_grad.astype(BF16)[None], loss[0, 0:1]
+    )(layer_map, boundaries, valid_counts, student_states, teacher_states, weights)
+    projector_grad = (pown + precv.astype(F32)).astype(BF16)
+    return gout[None], jnp.swapaxes(projector_grad, 0, 1)[None], loss[0, 0:1]
 
 
 def solution(mesh):

time: 219 us -> 190 us (0.87)
  Pallas kernels: 204 us -> 181 us
  local copies, waits for them, and re-layouts: 7.46 us -> 1.98 us
    pallas_call x1, Pallas kernels: 204 us -> 181 us  [per_device(): pl.pallas_call(kernel, out_shape=(jax.ShapeDtypeStruct((tokens, students)...]
    unnamed x4 -> x3, local copies, waits for them, and re-layouts: 6.12 us -> 0.8 us
    broadcast_in_dim x2 -> x1, other arithmetic: 5.8 us -> 4.5 us  [per_device(): return (gout[None], jnp.swapaxes(projector_grad, 0, 1)[None], loss[0, 0:1])]
where the time goes in v2:
time: 190 us; the launch traced here: 189 us
  Pallas kernels  181 us (95%)
  other arithmetic  4.5 us (2%)
  local copies, waits for them, and re-layouts  1.98 us (1%)
    pallas_call x1, Pallas kernels, per_device(): pl.pallas_call(kernel, out_shape=(jax.ShapeDtypeStruct((tokens, students)...  181 us
    broadcast_in_dim x1, other arithmetic, per_device(): return (gout[None], jnp.swapaxes(projector_grad, 0, 1)[None], loss[0, 0:1])  4.5 us

profile of v2, /device:TPU:6, one launch (start us, length us, event | category | flops | bytes accessed | tf_op | source)
XLA Modules:
  0.0 188.7 jit_solution(17003697935574974064)
XLA Ops:
  1.3 180.9 %shard_map.85 = (bf16[128,2048]{1,0:T(8,128)(2,1)}, f32[448,2048]{1,0:T(8,128)}, bf16[448,2048]{1,0:T(8,128)(2,1)}, f32[8,128]{1,0:T(8,128)}) custom-call(s32[16]{0:T(128)} %lm.1, s32[17]{0:T(128)} %bd.1, s32[1]{0:T(128)S(6)} %copy.10.vc, bf16[1,128,2048]{2,1,0:T(8,128)(2,1)} %x_hbm.1, bf16[4,128,7168]{2,1,0:T(8,128)(2,1)} %t_hbm.1, ...), custom_call_target="tpu_custom_call" | custom-call | tf_op jit(solution)/shard_map/pallas_call | solution.py:434
  182.2 1.2 slice.3
  183.4 0.0 copy-start
  183.4 4.5 %fusion = bf16[1,2048,448]{1,2,0:T(8,128)(2,1)} fusion(f32[448,2048]{1,0:T(8,128)} %get-tuple-element.8, bf16[448,2048]{1,0:T(8,128)(2,1)} %get-tuple-element.9), kind=kLoop, calls=%fused_computation.1 | loop fusion | flops 2752512 | bytes 7340032 | tf_op jit(solution)/shard_map/broadcast_in_dim | solution.py:495
  187.9 0.0 copy-done
  187.9 0.8 copy.11
Async XLA Ops:
  183.4 4.5 %copy-start = (bf16[128,2048]{1,0:T(8,128)(2,1)S(1)}, bf16[128,2048]{1,0:T(8,128)(2,1)}, u32[]{:S(2)}) copy-start(bf16[128,2048]{1,0:T(8,128)(2,1)} %get-tuple-element.7) | copy-start | bytes 1572868

commit v3 on v2

--- a/solution.py
+++ b/solution.py
@@ -24,8 +24,7 @@
     t_hbm,
     w_hbm,
     gout,
-    pown,
-    precv,
+    pout,
     loss,
     tv,
     blk,
@@ -40,9 +39,12 @@
     grads,
     xrecv,
     zsend,
-    zrecv,
-    gown,
+    acc,
     psend,
+    precv,
+    pown,
+    xex,
+    sex,
     cnt,
     lsum,
     sq,
@@ -69,6 +71,10 @@
     gz_rs,
     p_ss,
     p_rs,
+    xe_ss,
+    xe_rs,
+    se_ss,
+    se_rs,
     q_ss,
     q_rs,
 ):
@@ -89,8 +95,12 @@
     def z_at(k):
         return lax.rem(zl + k, N)
 
-    def z_back(k):
-        return lax.rem(zl + N - k, N)
+    upper = zl >= N // 2
+    inward = jnp.where(upper, N - 1 - zl, zl)
+
+    def place(s):
+        z = jnp.where(s == 0, 3, jnp.where(s == 1, 2, jnp.where(s == 2, 1 - inward, inward)))
+        return jnp.where(upper, N - 1 - z, z)
 
     def send(src, dst, ss, rs, where):
         copy = pltpu.make_async_remote_copy(
@@ -183,15 +193,15 @@
         owner = jnp.int32(0)
         for k in range(1, 16):
             owner = owner + jnp.where(bd[k] <= layer, 1, 0)
-        place = jnp.clip(layer - bd[here], 0, tv.shape[0] - 1)
-        return place, jnp.where(inside & (owner == here), F32(1.0), F32(0.0))
+        slot = jnp.clip(layer - bd[here], 0, tv.shape[0] - 1)
+        return slot, jnp.where(inside & (owner == here), F32(1.0), F32(0.0))
 
     def normalize(offset, dst):
-        place, keep = plan(offset)
+        slot, keep = plan(offset)
 
         def rows16(r, carry):
             rows = pl.ds(pl.multiple_of(r * 16, 16), 16)
-            h = tv[place, rows, :].astype(F32)
+            h = tv[slot, rows, :].astype(F32)
             scale = lax.rsqrt(jnp.mean(h * h, axis=1, keepdims=True) + norm_eps) * keep
             out = (h * scale).astype(BF16)
             for p in range(2):
@@ -228,9 +238,9 @@
         return carry
 
     lax.fori_loop(0, 2 * N, merge_far, 0)
-    order = [(q, k) for q in (1, 0) for k in (1, 2, 3, 0)]
-    for q, k in order:
-        i = chunk(q, z_at(k))
+    order = [(q, s) for s in range(N) for q in (1, 0)]
+    for q, s in order:
+        i = chunk(q, place(s))
         sent.append(
             send(blk.at[2 * zh, i], yrcv.at[i], y_ss.at[i], y_rs.at[i], {"y": y_to})
         )
@@ -242,34 +252,35 @@
         return carry
 
     lax.fori_loop(0, 2 * N, merge_near, 0)
-    for q, k in order:
-        i = chunk(q, z_at(k))
+    def near(n):
+        q, s = order[n]
+        i = chunk(q, place(s))
+        dst = tl.at[q * N + zl]
+        if (q, s) == (0, N - 1):
+            own = pltpu.make_async_copy(blk.at[1, i], dst, loc_sem.at[3])
+            own.start()
+            own.wait()
+        else:
+            where = {"x": xp if q else x, "zl": place(s)}
+            sent.append(send(blk.at[1, i], dst, l_ss.at[q * N + s], l_rs.at[q * N + zl], where))
+
+    near(0)
+    near(1)
+    for n, (q, s) in enumerate(order):
+        i = chunk(q, place(s))
         slot = q * N + zl
-        if (q, k) == (0, 0):
-            own = pltpu.make_async_copy(blk.at[1, i], tl.at[slot], loc_sem.at[3])
-            own.start()
-        else:
-            where = {"x": xp, "zl": z_at(k)} if q else {"zl": z_at(k)}
-            sent.append(send(blk.at[1, i], tl.at[slot], l_ss.at[q * N + k], l_rs.at[slot], where))
-
-    forward(2)
-
-    for q, k in order:
-        i = chunk(q, z_at(k))
         arrived(yrcv.at[i], y_ss.at[i], y_rs.at[i])
         merge(blk.at[2 * (1 - zh), i], yrcv.at[i])
-        where = {"zh": 1 - zh, "x": xp if q else x, "zl": z_at(k)}
+        where = {"zh": 1 - zh, "x": xp if q else x, "zl": place(s)}
         sent.append(
-            send(
-                blk.at[2 * (1 - zh), i],
-                tc.at[q * N + zl],
-                k_ss.at[q * N + k],
-                k_rs.at[q * N + zl],
-                where,
-            )
+            send(blk.at[2 * (1 - zh), i], tc.at[slot], k_ss.at[q * N + s], k_rs.at[slot], where)
         )
-
-    forward(3)
+        if n + 2 < 2 * N:
+            near(n + 2)
+        if n == 1:
+            forward(2)
+        if n == 3:
+            forward(3)
 
     for n, (kx, kz) in enumerate(others):
         d = lax.rem(x + kx, N) * N + z_at(kz)
@@ -282,15 +293,19 @@
     x_copy.wait()
     w_copy.wait()
     arrived(wpair.at[1 - half], w_ss, w_rs)
-    own.wait()
+    for z in range(N):
+        arrived(xall.at[N + z], xx_ss.at[z], x_rs.at[N + z])
+    for j in range(4):
+        slot = (1 - j % 2) * N + place(2 + j // 2)
+        sent.append(send(xall.at[slot], xex.at[j], xe_ss.at[j], xe_rs.at[j], {"x": wp}))
     sq[...] = jnp.zeros_like(sq)
 
-    def token_block(q, z):
+    def token_block(q, z, n):
         slot = q * N + z
-        d = (xp if q else x) * N + z
+        d = jnp.where(q == 1, xp, x) * N + z
         row = lax.broadcasted_iota(jnp.int32, (tokens, width), 0)
         valid = jnp.where(row < cnt[d, 0:1, 0:1], F32(1.0), F32(0.0))
-        base = pl.multiple_of(slot * tokens, tokens)
+        base = pl.multiple_of(n * tokens, tokens)
         nt = (((1,), (1,)), ((), ()))
         for e in range(2):
             at = slice(e * width, (e + 1) * width)
@@ -310,70 +325,162 @@
             )
             grads[slot, :, cols] = part.astype(BF16)
 
-    def far_block(k, carry):
-        z = lax.rem(zl + N - k - 1, N)
-        slot = N + z
-        arrived(xall.at[slot], xx_ss.at[z], x_rs.at[slot])
-        arrived(tl.at[slot], l_ss.at[slot], l_rs.at[slot])
+    step = 256
+
+    def outer(e, terms, cols):
+        value = None
+        for t, mine in terms:
+            if mine:
+                left_rows = sall[e, 2 * t * tokens : (2 * t + 2) * tokens, :]
+                blocks = [xall[N + place(t), :, cols], xall[place(t), :, cols]]
+            else:
+                left_rows = sex[2 * (t - 2) : 2 * (t - 1)].reshape(2 * tokens, width)
+                blocks = [xex[2 * (t - 2), :, cols], xex[2 * (t - 2) + 1, :, cols]]
+            part = lax.dot_general(
+                left_rows,
+                jnp.concatenate(blocks, axis=0),
+                (((0,), (0,)), ((), ())),
+                preferred_element_type=F32,
+            )
+            value = part if value is None else value + part
+        return value
+
+    def project(write):
+        def columns(j, carry):
+            write(pl.ds(pl.multiple_of(j * step, step), step))
+            return carry
+
+        lax.fori_loop(0, students // step, columns, 0)
+
+    def to_partner(cols):
+        psend[:, cols] = outer(1 - half, ((0, True), (1, True)), cols).astype(BF16)
+
+    def first_steps(cols):
+        terms = ((0, True), (1, True), (2, True), (2, False))
+        pown[:, cols] = outer(half, terms, cols)
+
+    def last_step(cols):
+        value = pown[:, cols] + precv[:, cols].astype(F32)
+        value = value + outer(half, ((3, True), (3, False)), cols)
+        pout[:, cols] = value.astype(BF16)
+
+    def extra_arrived(t):
+        for j in (2 * (t - 2), 2 * (t - 2) + 1):
+            arrived(xex.at[j], xe_ss.at[j], xe_rs.at[j])
+            arrived(sex.at[j], se_ss.at[j], se_rs.at[j])
+
+    def partner_piece(n):
+        return sall.at[1 - half, pl.ds(pl.multiple_of(n * tokens, tokens), tokens)]
+
+    def toward(s):
+        return jnp.where(place(s) > zl, 0, 1)
+
+    def add_rows(z, more, write):
+        def rows16(r, carry):
+            rows = pl.ds(pl.multiple_of(r * 16, 16), 16)
+            both = grads[z, rows, :].astype(F32) + xrecv[z, rows, :].astype(F32)
+            for way in more:
+                both = both + acc[way, z, rows, :].astype(F32)
+            write(rows, both.astype(BF16))
+            return carry
+
+        lax.fori_loop(0, tokens // 16, rows16, 0)
+
+    def along(s, act):
+        z, way = place(s), toward(s)
+        act(
+            zsend.at[s],
+            acc.at[way, z],
+            gz_ss.at[s],
+            gz_rs.at[way * N + z],
+            {"zl": zl + 1 - 2 * way},
+        )
+
+    def pass_on(s):
+        z, way = place(s), toward(s)
+        joined = jnp.where(way == 0, zl > 0, zl < N - 1)
+
+        def put(rows, value):
+            zsend[s, rows, :] = value
+
+        arrived(xrecv.at[z], gx_ss.at[z], gx_rs.at[z])
+
+        @pl.when(joined)
+        def _():
+            arrived(acc.at[way, z], gz_ss.at[s], gz_rs.at[way * N + z])
+            add_rows(z, (way,), put)
+
+        @pl.when(jnp.logical_not(joined))
+        def _():
+            add_rows(z, (), put)
+
+        along(s, send)
+
+    def one_block(n, carry):
+        s, q = lax.div(n, 2), 1 - lax.rem(n, 2)
+        z = place(s)
+        slot = q * N + z
+
+        @pl.when((q == 1) & (s > 0))
+        def _():
+            pass_on(s - 1)
+
+        @pl.when(n == 4)
+        def _():
+            project(to_partner)
+            send(psend, precv, p_ss, p_rs, {"x": wp})
+
+        @pl.when(n == 6)
+        def _():
+            extra_arrived(2)
+            project(first_steps)
+
+        @pl.when(n < 2 * N - 1)
+        def _():
+            arrived(tl.at[slot], l_ss.at[slot], l_rs.at[slot])
+
         arrived(tc.at[slot], k_ss.at[slot], k_rs.at[slot])
-        token_block(1, z)
-        send(grads.at[slot], xrecv.at[z], gx_ss.at[z], gx_rs.at[z], {"x": xp})
+        token_block(q, z, n)
+
+        @pl.when(q == 1)
+        def _():
+            send(grads.at[slot], xrecv.at[z], gx_ss.at[z], gx_rs.at[z], {"x": xp})
+
+        @pl.when(n >= 4)
+        def _():
+            send(partner_piece(n), sex.at[n - 4], se_ss.at[n - 4], se_rs.at[n - 4], {"x": wp})
+
         return carry
 
-    def near_block(k, carry):
-        z = lax.rem(zl + N - k - 1, N)
-
-        @pl.when(k < N - 1)
-        def _():
-            arrived(tl.at[z], l_ss.at[z], l_rs.at[z])
-
-        arrived(tc.at[z], k_ss.at[z], k_rs.at[z])
-        token_block(0, z)
-        return carry
-
-    lax.fori_loop(0, N, far_block, 0)
-    lax.fori_loop(0, N, near_block, 0)
+    lax.fori_loop(0, 2 * N, one_block, 0)
 
     lsum[me] = jnp.full(lsum.shape[1:], jnp.sum(sq[...]), F32)
     for n, (kx, kz) in enumerate(others):
         where = {"x": lax.rem(x + kx, N), "zl": z_at(kz)}
         sent.append(send(lsum.at[me], lsum.at[me], q_ss.at[n], q_rs.at[me], where))
 
-    step = 256
-
-    def project(e, dst):
-        def columns(j, carry):
-            cols = pl.ds(pl.multiple_of(j * step, step), step)
-            block = xall[:, :, cols].reshape(2 * N * tokens, step)
-            total_part = lax.dot_general(
-                sall[e], block, (((0,), (0,)), ((), ())), preferred_element_type=F32
-            )
-            dst[:, cols] = total_part.astype(dst.dtype)
-            return carry
-
-        lax.fori_loop(0, students // step, columns, 0)
-
-    project(1 - half, psend)
-    sent.append(send(psend, precv, p_ss, p_rs, {"x": wp}))
-
-    def summed(z, dst):
-        def rows16(r, carry):
-            rows = pl.ds(pl.multiple_of(r * 16, 16), 16)
-            both = grads[z, rows, :].astype(F32) + xrecv[z, rows, :].astype(F32)
-            dst[rows, :] = both.astype(dst.dtype)
-            return carry
-
-        arrived(xrecv.at[z], gx_ss.at[z], gx_rs.at[z])
-        lax.fori_loop(0, tokens // 16, rows16, 0)
-
-    for k in (1, 2, 3):
-        z = z_back(k)
-        summed(z, zsend.at[k - 1])
-        sent.append(
-            send(zsend.at[k - 1], zrecv.at[N - 1 - k], gz_ss.at[k - 1], gz_rs.at[N - 1 - k], {"zl": z})
-        )
-    project(half, pown)
-    summed(zl, gown)
+    arrived(precv, p_ss, p_rs)
+    extra_arrived(3)
+    project(last_step)
+
+    def put_out(rows, value):
+        gout[rows, :] = value
+
+    arrived(xrecv.at[zl], gx_ss.at[zl], gx_rs.at[zl])
+
+    @pl.when(zl > 0)
+    def _():
+        arrived(acc.at[0, zl], gz_ss.at[0], gz_rs.at[zl])
+
+    @pl.when(zl < N - 1)
+    def _():
+        arrived(acc.at[1, zl], gz_ss.at[0], gz_rs.at[N + zl])
+
+    for low, high, ways in ((0, 1, (1,)), (1, N - 1, (0, 1)), (N - 1, N, (0,))):
+
+        @pl.when((zl >= low) & (zl < high))
+        def _():
+            add_rows(zl, ways, put_out)
 
     for n, (kx, kz) in enumerate(others):
         d = lax.rem(x + kx, N) * N + z_at(kz)
@@ -381,21 +488,7 @@
     squares = lsum[0]
     for d in range(1, N * N):
         squares = squares + lsum[d]
-    loss[...] = squares / (total * rest)
-
-    for k in range(3):
-        arrived(zrecv.at[k], gz_ss.at[k], gz_rs.at[k])
-
-    def result(r, carry):
-        rows = pl.ds(pl.multiple_of(r * 16, 16), 16)
-        value = gown[rows, :]
-        for k in range(3):
-            value = value + zrecv[k, rows, :].astype(F32)
-        gout[rows, :] = value.astype(BF16)
-        return carry
-
-    lax.fori_loop(0, tokens // 16, result, 0)
-    arrived(precv, p_ss, p_rs)
+    loss[0] = jnp.max(squares / (total * rest))
 
     def drain(src, dst, ss, rs, where):
         pltpu.make_async_remote_copy(
@@ -414,6 +507,11 @@
         return carry
 
     lax.fori_loop(0, N, far_sent, 0)
+    drain(psend, precv, p_ss, p_rs, {"x": wp})
+    for s in range(3):
+        along(s, drain)
+    for n in range(4, 2 * N):
+        drain(partner_piece(n), sex.at[n - 4], se_ss.at[n - 4], se_rs.at[n - 4], {"x": wp})
     for copy in sent:
         copy.wait_send()
 
@@ -431,16 +529,15 @@
     vmem = pl.BlockSpec(memory_space=pltpu.VMEM)
     dma = pltpu.SemaphoreType.DMA
     piece = (2 * N, tokens, 2 * width)
-    gout, pown, precv, loss = pl.pallas_call(
+    gout, pout, loss = pl.pallas_call(
         kernel,
         out_shape=(
             jax.ShapeDtypeStruct((tokens, students), BF16),
-            jax.ShapeDtypeStruct((width, students), F32),
             jax.ShapeDtypeStruct((width, students), BF16),
-            jax.ShapeDtypeStruct((8, 128), F32),
+            jax.ShapeDtypeStruct((1,), F32),
         ),
         in_specs=[smem, smem, smem, any_space, any_space, any_space],
-        out_specs=(vmem, vmem, any_space, vmem),
+        out_specs=(vmem, vmem, smem),
         scratch_shapes=[
             pltpu.VMEM((slots, tokens, features), BF16),
             pltpu.VMEM((3, *piece), BF16),
@@ -455,9 +552,12 @@
             pltpu.VMEM((2 * N, tokens, students), BF16),
             pltpu.VMEM((N, tokens, students), BF16),
             pltpu.VMEM((3, tokens, students), BF16),
-            pltpu.VMEM((3, tokens, students), BF16),
-            pltpu.VMEM((tokens, students), F32),
+            pltpu.VMEM((2, N, tokens, students), BF16),
             pltpu.VMEM((width, students), BF16),
+            pltpu.VMEM((width, students), BF16),
+            pltpu.VMEM((width, students), F32),
+            pltpu.VMEM((4, tokens, students), BF16),
+            pltpu.VMEM((4, tokens, width), BF16),
             pltpu.VMEM((N * N, 8, 128), jnp.int32),
             pltpu.VMEM((N * N, 8, 128), F32),
             pltpu.VMEM((1, width), F32),
@@ -481,9 +581,13 @@
             dma((N,)),
             dma((N,)),
             dma((3,)),
-            dma((3,)),
+            dma((2 * N,)),
             dma,
             dma,
+            dma((4,)),
+            dma((4,)),
+            dma((4,)),
+            dma((4,)),
             dma((16,)),
             dma((16,)),
         ],
@@ -491,8 +595,7 @@
             collective_id=0, has_side_effects=True, vmem_limit_bytes=67043328
         ),
     )(layer_map, boundaries, valid_counts, student_states, teacher_states, weights)
-    projector_grad = (pown + precv.astype(F32)).astype(BF16)
-    return gout[None], jnp.swapaxes(projector_grad, 0, 1)[None], loss[0, 0:1]
+    return gout[None], jnp.swapaxes(pout, 0, 1)[None], loss
 
 
 def solution(mesh):

time: 190 us -> 221 us (1.16)
  Pallas kernels: 181 us -> 210 us
  other arithmetic: 4.5 us -> 0 us
  local copies, waits for them, and re-layouts: 1.98 us -> 4.82 us
    pallas_call x1, Pallas kernels: 181 us -> 210 us  [per_device(): pl.pallas_call(kernel, out_shape=(jax.ShapeDtypeStruct((tokens, students)...]
    broadcast_in_dim x1 -> x0, other arithmetic: 4.5 us -> none  [per_device(): return (gout[None], jnp.swapaxes(projector_grad, 0, 1)[None], loss[0, 0:1])]
    unnamed x3 -> x2, local copies, waits for them, and re-layouts: 0.8 us -> 4.82 us
where the time goes in v3:
time: 221 us; the launch traced here: 218 us
  Pallas kernels  210 us (95%)
  local copies, waits for them, and re-layouts  4.82 us (2%)
  between operations  3.04 us (1%)
    pallas_call x1, Pallas kernels, per_device(): pl.pallas_call(kernel, out_shape=(jax.ShapeDtypeStruct((tokens, students)...  210 us
    unnamed x2, local copies, waits for them, and re-layouts  4.82 us

profile of v3, /device:TPU:6, one launch (start us, length us, event | category | flops | bytes accessed | tf_op | source)
XLA Modules:
  0.0 217.6 jit_solution(12265884788737264481)
XLA Ops:
  1.3 209.8 %shard_map.85 = (bf16[128,2048]{1,0:T(8,128)(2,1)}, bf16[448,2048]{1,0:T(8,128)(2,1)}, f32[1]{0:T(128)}) custom-call(s32[16]{0:T(128)} %lm.1, s32[17]{0:T(128)} %bd.1, s32[1]{0:T(128)S(6)} %copy.12.vc, bf16[1,128,2048]{2,1,0:T(8,128)(2,1)} %x_hbm.1, bf16[4,128,7168]{2,1,0:T(8,128)(2,1)} %t_hbm.1, bf16[1,448,2048]{2,1,0:T(8,128)(2,1)} %bitcast.5), custom_call_target="tpu_custom_call" | custom-call | tf_op jit(solution)/shard_map/pallas_call | solution.py:532
  211.1 1.9 copy.13
  213.0 2.9 %copy.14 = bf16[1,2048,448]{1,2,0:T(8,128)(2,1)} copy(bf16[1,2048,448]{1,2,0:T(8,128)(2,1)} %bitcast.6) | data formatting | bytes 3670016

commit v4 on v3

--- a/solution.py
+++ b/solution.py
@@ -178,6 +178,11 @@
 
         from_right(j, send)
 
+    def extra(j):
+        slot = (1 - j % 2) * N + place(2 + j // 2)
+        block = x_hbm.at[0] if j == 3 else xall.at[slot]
+        sent.append(send(block, xex.at[j], xe_ss.at[j], xe_rs.at[j], {"x": wp}))
+
     right(zl, send)
     left(zl, send)
     across(zl, send)
@@ -229,6 +234,8 @@
         normalize(offset, snd.at[n])
         sent.append(send(snd.at[n], rcv.at[n], d_ss.at[n], d_rs.at[n], {"c": 1 - c}))
     forward(1)
+    extra(3)
+    extra(1)
     normalize(-2, blk.at[0])
     normalize(2, blk.at[2])
     arrived(rcv.at[1 - c], d_ss.at[1 - c], d_rs.at[1 - c])
@@ -281,6 +288,10 @@
             forward(2)
         if n == 3:
             forward(3)
+            for j in (2, 0):
+                z = place(2 + j // 2)
+                arrived(xall.at[N + z], xx_ss.at[z], x_rs.at[N + z])
+                extra(j)
 
     for n, (kx, kz) in enumerate(others):
         d = lax.rem(x + kx, N) * N + z_at(kz)
@@ -293,11 +304,6 @@
     x_copy.wait()
     w_copy.wait()
     arrived(wpair.at[1 - half], w_ss, w_rs)
-    for z in range(N):
-        arrived(xall.at[N + z], xx_ss.at[z], x_rs.at[N + z])
-    for j in range(4):
-        slot = (1 - j % 2) * N + place(2 + j // 2)
-        sent.append(send(xall.at[slot], xex.at[j], xe_ss.at[j], xe_rs.at[j], {"x": wp}))
     sq[...] = jnp.zeros_like(sq)
 
     def token_block(q, z, n):
@@ -356,12 +362,12 @@
         psend[:, cols] = outer(1 - half, ((0, True), (1, True)), cols).astype(BF16)
 
     def first_steps(cols):
-        terms = ((0, True), (1, True), (2, True), (2, False))
+        terms = ((0, True), (1, True), (2, True))
         pown[:, cols] = outer(half, terms, cols)
 
     def last_step(cols):
         value = pown[:, cols] + precv[:, cols].astype(F32)
-        value = value + outer(half, ((3, True), (3, False)), cols)
+        value = value + outer(half, ((3, True), (2, False), (3, False)), cols)
         pout[:, cols] = value.astype(BF16)
 
     def extra_arrived(t):
@@ -421,10 +427,6 @@
         z = place(s)
         slot = q * N + z
 
-        @pl.when((q == 1) & (s > 0))
-        def _():
-            pass_on(s - 1)
-
         @pl.when(n == 4)
         def _():
             project(to_partner)
@@ -432,12 +434,15 @@
 
         @pl.when(n == 6)
         def _():
-            extra_arrived(2)
             project(first_steps)
 
         @pl.when(n < 2 * N - 1)
         def _():
             arrived(tl.at[slot], l_ss.at[slot], l_rs.at[slot])
+
+        @pl.when((q == 1) & (s < 2))
+        def _():
+            arrived(xall.at[slot], xx_ss.at[z], x_rs.at[slot])
 
         arrived(tc.at[slot], k_ss.at[slot], k_rs.at[slot])
         token_block(q, z, n)
@@ -459,7 +464,10 @@
         where = {"x": lax.rem(x + kx, N), "zl": z_at(kz)}
         sent.append(send(lsum.at[me], lsum.at[me], q_ss.at[n], q_rs.at[me], where))
 
+    for s in range(3):
+        pass_on(s)
     arrived(precv, p_ss, p_rs)
+    extra_arrived(2)
     extra_arrived(3)
     project(last_step)
 

time: 221 us -> 177 us (0.80)
  Pallas kernels: 210 us -> 167 us
    pallas_call x1, Pallas kernels: 210 us -> 167 us  [per_device(): pl.pallas_call(kernel, out_shape=(jax.ShapeDtypeStruct((tokens, students)...]
where the time goes in v4:
time: 177 us; the launch traced here: 175 us
  Pallas kernels  167 us (94%)
  local copies, waits for them, and re-layouts  4.82 us (3%)
  between operations  3.04 us (2%)
    pallas_call x1, Pallas kernels, per_device(): pl.pallas_call(kernel, out_shape=(jax.ShapeDtypeStruct((tokens, students)...  167 us
    unnamed x2, local copies, waits for them, and re-layouts  4.82 us

profile of v4, /device:TPU:6, one launch (start us, length us, event | category | flops | bytes accessed | tf_op | source)
XLA Modules:
  0.0 175.3 jit_solution(17407652012295885637)
XLA Ops:
  1.3 167.4 %shard_map.85 = (bf16[128,2048]{1,0:T(8,128)(2,1)}, bf16[448,2048]{1,0:T(8,128)(2,1)}, f32[1]{0:T(128)}) custom-call(s32[16]{0:T(128)} %lm.1, s32[17]{0:T(128)} %bd.1, s32[1]{0:T(128)S(6)} %copy.12.vc, bf16[1,128,2048]{2,1,0:T(8,128)(2,1)} %x_hbm.1, bf16[4,128,7168]{2,1,0:T(8,128)(2,1)} %t_hbm.1, bf16[1,448,2048]{2,1,0:T(8,128)(2,1)} %bitcast.5), custom_call_target="tpu_custom_call" | custom-call | tf_op jit(solution)/shard_map/pallas_call | solution.py:540
  168.7 1.9 %copy.13 = bf16[1,128,2048]{2,1,0:T(8,128)(2,1)} copy(bf16[1,128,2048]{2,1,0:T(8,128)(2,1)} %bitcast.7) | data formatting | bytes 1048576
  170.6 2.9 %copy.14 = bf16[1,2048,448]{1,2,0:T(8,128)(2,1)} copy(bf16[1,2048,448]{1,2,0:T(8,128)(2,1)} %bitcast.6) | data formatting | bytes 3670016

commit v5 on v4

--- a/solution.py
+++ b/solution.py
@@ -95,6 +95,12 @@
     def z_at(k):
         return lax.rem(zl + k, N)
 
+    def goal(s):
+        return lax.rem(zl + s + 1, N)
+
+    def source(s):
+        return lax.rem(zl + 3 - s, N)
+
     upper = zl >= N // 2
     inward = jnp.where(upper, N - 1 - zl, zl)
 
@@ -178,10 +184,10 @@
 
         from_right(j, send)
 
-    def extra(j):
-        slot = (1 - j % 2) * N + place(2 + j // 2)
+    def extra(j, act):
+        slot = (1 - j % 2) * N + source(2 + j // 2)
         block = x_hbm.at[0] if j == 3 else xall.at[slot]
-        sent.append(send(block, xex.at[j], xe_ss.at[j], xe_rs.at[j], {"x": wp}))
+        act(block, xex.at[j], xe_ss.at[j], xe_rs.at[j], {"x": wp})
 
     right(zl, send)
     left(zl, send)
@@ -234,8 +240,7 @@
         normalize(offset, snd.at[n])
         sent.append(send(snd.at[n], rcv.at[n], d_ss.at[n], d_rs.at[n], {"c": 1 - c}))
     forward(1)
-    extra(3)
-    extra(1)
+    extra(3, send)
     normalize(-2, blk.at[0])
     normalize(2, blk.at[2])
     arrived(rcv.at[1 - c], d_ss.at[1 - c], d_rs.at[1 - c])
@@ -247,7 +252,7 @@
     lax.fori_loop(0, 2 * N, merge_far, 0)
     order = [(q, s) for s in range(N) for q in (1, 0)]
     for q, s in order:
-        i = chunk(q, place(s))
+        i = chunk(q, goal(s))
         sent.append(
             send(blk.at[2 * zh, i], yrcv.at[i], y_ss.at[i], y_rs.at[i], {"y": y_to})
         )
@@ -261,24 +266,24 @@
     lax.fori_loop(0, 2 * N, merge_near, 0)
     def near(n):
         q, s = order[n]
-        i = chunk(q, place(s))
+        i = chunk(q, goal(s))
         dst = tl.at[q * N + zl]
         if (q, s) == (0, N - 1):
             own = pltpu.make_async_copy(blk.at[1, i], dst, loc_sem.at[3])
             own.start()
             own.wait()
         else:
-            where = {"x": xp if q else x, "zl": place(s)}
+            where = {"x": xp if q else x, "zl": goal(s)}
             sent.append(send(blk.at[1, i], dst, l_ss.at[q * N + s], l_rs.at[q * N + zl], where))
 
     near(0)
     near(1)
     for n, (q, s) in enumerate(order):
-        i = chunk(q, place(s))
+        i = chunk(q, goal(s))
         slot = q * N + zl
         arrived(yrcv.at[i], y_ss.at[i], y_rs.at[i])
         merge(blk.at[2 * (1 - zh), i], yrcv.at[i])
-        where = {"zh": 1 - zh, "x": xp if q else x, "zl": place(s)}
+        where = {"zh": 1 - zh, "x": xp if q else x, "zl": goal(s)}
         sent.append(
             send(blk.at[2 * (1 - zh), i], tc.at[slot], k_ss.at[q * N + s], k_rs.at[slot], where)
         )
@@ -288,10 +293,9 @@
             forward(2)
         if n == 3:
             forward(3)
-            for j in (2, 0):
-                z = place(2 + j // 2)
-                arrived(xall.at[N + z], xx_ss.at[z], x_rs.at[N + z])
-                extra(j)
+            extra(1, send)
+            arrived(xall.at[N + zl], xx_ss.at[zl], x_rs.at[N + zl])
+            extra(2, send)
 
     for n, (kx, kz) in enumerate(others):
         d = lax.rem(x + kx, N) * N + z_at(kz)
@@ -338,7 +342,7 @@
         for t, mine in terms:
             if mine:
                 left_rows = sall[e, 2 * t * tokens : (2 * t + 2) * tokens, :]
-                blocks = [xall[N + place(t), :, cols], xall[place(t), :, cols]]
+                blocks = [xall[N + source(t), :, cols], xall[source(t), :, cols]]
             else:
                 left_rows = sex[2 * (t - 2) : 2 * (t - 1)].reshape(2 * tokens, width)
                 blocks = [xex[2 * (t - 2), :, cols], xex[2 * (t - 2) + 1, :, cols]]
@@ -424,11 +428,13 @@
 
     def one_block(n, carry):
         s, q = lax.div(n, 2), 1 - lax.rem(n, 2)
-        z = place(s)
+        z = source(s)
         slot = q * N + z
 
         @pl.when(n == 4)
         def _():
+            arrived(xall.at[slot], xx_ss.at[z], x_rs.at[slot])
+            extra(0, send)
             project(to_partner)
             send(psend, precv, p_ss, p_rs, {"x": wp})
 
@@ -518,6 +524,8 @@
     drain(psend, precv, p_ss, p_rs, {"x": wp})
     for s in range(3):
         along(s, drain)
+    for j in range(4):
+        extra(j, drain)
     for n in range(4, 2 * N):
         drain(partner_piece(n), sex.at[n - 4], se_ss.at[n - 4], se_rs.at[n - 4], {"x": wp})
     for copy in sent:

time: 177 us -> 193 us (1.090)
  Pallas kernels: 167 us -> 183 us
    pallas_call x1, Pallas kernels: 167 us -> 183 us  [per_device(): pl.pallas_call(kernel, out_shape=(jax.ShapeDtypeStruct((tokens, students)...]
where the time goes in v5:
time: 193 us; the launch traced here: 191 us
  Pallas kernels  183 us (95%)
  local copies, waits for them, and re-layouts  4.82 us (2%)
  between operations  3.04 us (2%)
    pallas_call x1, Pallas kernels, per_device(): pl.pallas_call(kernel, out_shape=(jax.ShapeDtypeStruct((tokens, students)...  183 us
    unnamed x2, local copies, waits for them, and re-layouts  4.82 us

profile of v5, /device:TPU:6, one launch (start us, length us, event | category | flops | bytes accessed | tf_op | source)
XLA Modules:
  0.0 190.9 jit_solution(4209474020027993964)
XLA Ops:
  1.3 183.1 %shard_map.85 = (bf16[128,2048]{1,0:T(8,128)(2,1)}, bf16[448,2048]{1,0:T(8,128)(2,1)}, f32[1]{0:T(128)}) custom-call(s32[16]{0:T(128)} %lm.1, s32[17]{0:T(128)} %bd.1, s32[1]{0:T(128)S(6)} %copy.12.vc, bf16[1,128,2048]{2,1,0:T(8,128)(2,1)} %x_hbm.1, bf16[4,128,7168]{2,1,0:T(8,128)(2,1)} %t_hbm.1, bf16[1,448,2048]{2,1,0:T(8,128)(2,1)} %bitcast.5), custom_call_target="tpu_custom_call" | custom-call | tf_op jit(solution)/shard_map/pallas_call | solution.py:548
  184.3 1.9 copy.13
  186.2 2.9 %copy.14 = bf16[1,2048,448]{1,2,0:T(8,128)(2,1)} copy(bf16[1,2048,448]{1,2,0:T(8,128)(2,1)} %bitcast.6) | data formatting | bytes 3670016
